TPU v7x, 32 devices: a whole 2x2x4 slice. The times are simulated.
32 devices in a mesh: groups: 2 (over y), seq: 4 (over z), exp: 2 (over x), tp: 2 (over core).
Axes of the slice: x: 2, y: 2, z: 4, core: 2. Of those that a mesh axis runs over, the one named last changes fastest.
Arguments:
- attn_query: bfloat16 [2048, 1152], P(('groups', 'seq'), ('exp', 'tp')), parts along dimension 0, may hold values from -6 to 6
- fresh_keys: bfloat16 [2048, 1152], P(('groups', 'seq'), ('exp', 'tp')), parts along dimension 0, may hold values from -6 to 6
- fresh_values: bfloat16 [2048, 1152], P(('groups', 'seq'), ('exp', 'tp')), parts along dimension 0, may hold values from -6 to 6
- stale_keys: bfloat16 [2048, 1152], P(('groups', 'seq'), ('exp', 'tp')), parts along dimension 0, may hold values from -6 to 6
- stale_values: bfloat16 [2048, 1152], P(('groups', 'seq'), ('exp', 'tp')), parts along dimension 0, may hold values from -6 to 6
- block_flags: int32 [16], P(('groups', 'seq')), parts along dimension 0, may hold values 0 or 1
- moe_tokens: bfloat16 [4096, 1152], P(('groups', 'seq', 'exp', 'tp')), parts along dimension 0, may hold values from -6 to 6
- expert_ids: int32 [4096, 2], P(('groups', 'seq', 'exp', 'tp')), parts along dimension 0, may hold values from 0 to 3, all different within a row; in each aligned block of 128 rows (0 to 127, 128 to 255, ...) at most 80 rows name the same one
- gate_weights: float32 [4096, 2], P(('groups', 'seq', 'exp', 'tp')), parts along dimension 0, may hold values from 0.25 to 1
- up_weight: bfloat16 [4, 1152, 4608], P('seq', None, ('exp', 'tp')), may hold values from -0.1875 to 0.1875
- up_bias: float32 [4, 4608], P('seq', ('exp', 'tp')), may hold values from -3 to 3
- down_weight: bfloat16 [4, 4608, 1152], P('seq', ('exp', 'tp')), may hold values from -0.09375 to 0.09375
- down_bias: float32 [4, 1152], P('seq'), may hold values from -2 to 2
Outputs:
- attn_out: bfloat16 [2048, 1152], P(('groups', 'seq'), ('exp', 'tp')), parts along dimension 0
- moe_out: bfloat16 [4096, 1152], P(('groups', 'seq', 'exp', 'tp')), parts along dimension 0
There are 2 independent parts, one for each index of `groups`. A program takes and returns all parts, laid end to end along the dimension named above; an argument that names none is the same for every part. Nothing has to cross between parts.
Inputs may be any that keep to these rules, and one draw needn't show every extreme that they name: `expert_ids`: the 2 ids of a token differ. In the rows of one device no expert is named more than 80 times, and in every draw some expert is named exactly 80 times in some device's rows.
All inputs are finite; a program needn't handle non-finite values. No bound on the sum of `block_flags` on one device may be relied on, other than what follows from the above.
Results may differ from a plain program's by a relative error of at most 0.014.
Values may be sent and summed in bfloat16 or wider, within the bound.
A program may use at most 64 MiB of HBM per device.

v0:
```python
import math
import jax
import jax.numpy as jnp
from jax import lax
from jax.sharding import PartitionSpec as P

HD = 72


def over_all_2(share, axis, dim, apply):
    everything = lax.all_gather(share, axis, axis=dim, tiled=True)
    return apply(everything, jnp.int32(0))


def attention_part(attn_query, fresh_keys, fresh_values, stale_keys, stale_values, block_flags):
    length = attn_query.shape[0]
    heads_here = attn_query.shape[1] // HD
    row_flags = (jnp.repeat(block_flags, length // block_flags.shape[0]) == 1)[:, None]
    keys = jnp.where(row_flags, fresh_keys, stale_keys)
    values = jnp.where(row_flags, fresh_values, stale_values)
    queries = attn_query.reshape(length, heads_here, HD)
    scale = 1.0 / math.sqrt(HD)
    initial = (
        jnp.full((heads_here, length), -1e30, jnp.float32),
        jnp.zeros((heads_here, length), jnp.float32),
        jnp.zeros((heads_here, length, HD), jnp.float32),
    )
    carry = initial
    piece = (
        lax.all_gather(keys, "seq", axis=0, tiled=True),
        lax.all_gather(values, "seq", axis=0, tiled=True),
    )
    count = piece[0].shape[0]
    width = math.gcd(count, 512)
    key_blocks = piece[0].reshape(count // width, width, heads_here, HD)
    value_blocks = piece[1].reshape(count // width, width, heads_here, HD)

    def advance(state, blocks):
        highest, totals, weighted = state
        key_block, value_block = blocks
        scores = (
            jnp.einsum("qhd,khd->hqk", queries, key_block, preferred_element_type=jnp.float32)
            * scale
        )
        new_high = jnp.maximum(highest, jnp.max(scores, axis=-1))
        rescale = jnp.exp(highest - new_high)
        probs = jnp.exp(scores - new_high[:, :, None])
        totals = totals * rescale + jnp.sum(probs, axis=-1)
        weighted = weighted * rescale[:, :, None] + jnp.einsum(
            "hqk,khd->hqd",
            probs.astype(jnp.bfloat16),
            value_block,
            preferred_element_type=jnp.float32,
        )
        return ((new_high, totals, weighted), None)

    carry, unused = lax.scan(advance, carry, (key_blocks, value_blocks))
    highest, totals, weighted = carry
    mixed = weighted / totals[:, :, None]
    return jnp.transpose(mixed, (1, 0, 2)).reshape(length, heads_here * HD).astype(jnp.bfloat16)


def expert_part(moe_tokens, expert_ids, gate_weights, up_weight, up_bias, down_weight, down_bias):
    tokens_here, width = moe_tokens.shape
    choose = expert_ids.shape[1]
    number = lax.axis_size("seq") * up_weight.shape[0]
    capacity = 5 * tokens_here // (2 * number)
    flat_ids = expert_ids.reshape(-1)
    hits = (flat_ids[:, None] == jnp.arange(number, dtype=jnp.int32)[None, :]).astype(jnp.int32)
    before = jnp.cumsum(hits, axis=0) - hits
    place = jnp.sum(before * hits, axis=1)
    slot = flat_ids * capacity + place
    slot_pairs = slot.reshape(tokens_here, choose)
    table = jnp.sum(
        (
            slot_pairs[None, :, :] == jnp.arange(number * capacity, dtype=jnp.int32)[:, None, None]
        ).astype(jnp.int32),
        axis=-1,
    )
    buffer = jnp.dot(
        table.astype(jnp.bfloat16), moe_tokens, preferred_element_type=jnp.float32
    ).astype(jnp.bfloat16)
    buffer = buffer.reshape(number, capacity, width)
    received = lax.all_to_all(buffer, "seq", split_axis=0, concat_axis=0, tiled=True)
    sources = received.shape[0]
    count = received.shape[1]
    flat_rows = received.reshape(sources * count, width)
    chip_rows = lax.all_gather(flat_rows, "tp", axis=0, tiled=True)

    def project(piece):
        return jax.nn.gelu(
            jnp.dot(chip_rows, piece[0], preferred_element_type=jnp.float32) + piece[1]
        ).astype(jnp.bfloat16)

    hidden = over_all_2(
        (up_weight[0], up_bias[0][None, :].astype(jnp.bfloat16)),
        "exp",
        1,
        lambda piece, start: project((piece[0], piece[1].astype(jnp.float32))),
    )
    down_whole = lax.all_gather(down_weight[0], "exp", axis=0, tiled=True)
    summed = lax.psum_scatter(
        jnp.dot(hidden, down_whole, preferred_element_type=jnp.float32).astype(jnp.bfloat16),
        "tp",
        scatter_dimension=0,
        tiled=True,
    ).astype(jnp.float32)
    result = (summed + down_bias[0][None, :]).astype(jnp.bfloat16).reshape(sources, count, width)
    returned = lax.all_to_all(result, "seq", split_axis=0, concat_axis=0, tiled=True)
    flat_out = returned.reshape(number * capacity, width)
    picked = flat_out[slot].reshape(tokens_here, choose, width).astype(jnp.float32)
    combined = jnp.sum(picked * gate_weights[:, :, None], axis=1)
    return combined.astype(jnp.bfloat16)


def local(
    attn_query,
    fresh_keys,
    fresh_values,
    stale_keys,
    stale_values,
    block_flags,
    moe_tokens,
    expert_ids,
    gate_weights,
    up_weight,
    up_bias,
    down_weight,
    down_bias,
):
    attn_out = attention_part(
        attn_query, fresh_keys, fresh_values, stale_keys, stale_values, block_flags
    )
    moe_out = expert_part(
        moe_tokens, expert_ids, gate_weights, up_weight, up_bias, down_weight, down_bias
    )
    return (attn_out, moe_out)


def solution(mesh):
    in_specs = (
        P(("groups", "seq"), ("exp", "tp")),
        P(("groups", "seq"), ("exp", "tp")),
        P(("groups", "seq"), ("exp", "tp")),
        P(("groups", "seq"), ("exp", "tp")),
        P(("groups", "seq"), ("exp", "tp")),
        P(("groups", "seq")),
        P(("groups", "seq", "exp", "tp"), None),
        P(("groups", "seq", "exp", "tp"), None),
        P(("groups", "seq", "exp", "tp"), None),
        P("seq", None, ("exp", "tp")),
        P("seq", ("exp", "tp")),
        P("seq", ("exp", "tp"), None),
        P("seq", None),
    )
    out_specs = (P(("groups", "seq"), ("exp", "tp")), P(("groups", "seq", "exp", "tp"), None))
    return jax.shard_map(local, mesh=mesh, in_specs=in_specs, out_specs=out_specs, check_vma=False)
```

profile of v0, /device:TPU:0, one launch (start us, length us, event | category | flops | bytes accessed | tf_op | source)
XLA Modules:
  0.0 262.1 jit_solution(10440550585438227936)
XLA Ops:
  7.2 0.8 copy.32
  8.3 1.2 reduce-window.6
  10.3 0.3 convolution_convert_fusion
  10.6 25.3 %all_to_all.10 = bf16[4,80,1152]{2,1,0:T(8,128)(2,1)} all-to-all(bf16[4,80,1152]{2,1,0:T(8,128)(2,1)S(1)} %bitcast.82), channel_id=1, replica_groups=mesh['groups'=2,'seq'=4,'exp'=2,'tp'=2] {'seq'}, dimensions={0} | all-to-all | bytes 1474560 | tf_op jit(solution)/shard_map/all_to_all | solution.py:84
  36.0 0.7 all-gather.8.cloned.1.call-update
  36.8 0.7 all-gather.10.cloned.1.call-update
  37.5 4.4 %all_gather.22 = bf16[1,2304]{1,0:T(2,128)(2,1)S(1)} all-gather(bf16[1,1152]{1,0:T(2,128)(2,1)S(1)} %convert_element_type.61), channel_id=1, replica_groups=mesh['groups'=2,'seq'=4,'exp'=2,'tp'=2] {'exp'}, dimensions={1}, use_global_device_ids=true | all-gather | bytes 6912 | tf_op jit(solution)/shard_map/all_gather | solution.py:11
  41.9 3.0 %all-gather.6.cloned.1.call-done = bf16[640,1152]{1,0:T(8,128)(2,1)} async-done(((bf16[320,1152]{1,0:T(8,128)(2,1)}), bf16[640,1152]{1,0:T(8,128)(2,1)}) %all-gather.6.cloned.1.call-update) | async-done | bytes 1474576 | tf_op jit(solution)/shard_map/all_gather | solution.py:88
  44.9 72.0 %all-gather.8.cloned.1.call-done = bf16[1,1152,2304]{2,1,0:T(8,128)(2,1)} async-done(((bf16[1,1152,1152]{2,1,0:T(8,128)(2,1)}), bf16[1,1152,2304]{2,1,0:T(8,128)(2,1)}) %all-gather.8.cloned.1.call-update) | async-done | bytes 5308432 | tf_op jit(solution)/shard_map/all_gather | solution.py:11
  116.9 9.6 %fusion.22 = bf16[640,2304]{1,0:T(8,128)(2,1)} fusion(bf16[640,1152]{1,0:T(8,128)(2,1)} %all-gather.6.cloned.1.call-done, bf16[1,1152,2304]{2,1,0:T(8,128)(2,1)} %all-gather.8.cloned.1.call-done, f32[2304]{0:T(1024)S(1)} %convert_reduce_fusion.1), kind=kOutput, calls=%fused_computation.30 | convolution fusion | flops 3412131840 | bytes 9741312 | tf_op jit(solution)/shard_map/dot_general | solution.py:92
  126.5 61.3 %all-gather.10.cloned.1.call-done = bf16[1,2304,1152]{2,1,0:T(8,128)(2,1)} async-done(((bf16[1,1152,1152]{2,1,0:T(8,128)(2,1)}), bf16[1,2304,1152]{2,1,0:T(8,128)(2,1)}) %all-gather.10.cloned.1.call-update) | async-done | bytes 5308432 | tf_op jit(solution)/shard_map/all_gather | solution.py:101
  187.8 8.5 %fusion.29 = bf16[640,1152]{1,0:T(8,128)(2,1)} fusion(bf16[640,2304]{1,0:T(8,128)(2,1)} %fusion.22, bf16[1,2304,1152]{2,1,0:T(8,128)(2,1)} %all-gather.10.cloned.1.call-done), kind=kOutput, calls=%fused_computation.35 | convolution fusion | flops 3398123520 | bytes 9732096 | tf_op jit(solution)/shard_map/dot_general | solution.py:103
  196.5 16.5 %all_gather.18 = bf16[1024,288]{0,1:T(8,128)(2,1)S(1)} all-gather(bf16[256,288]{0,1:T(8,128)(2,1)S(1)} %get-tuple-element.101), channel_id=1, replica_groups=mesh['groups'=2,'seq'=4,'exp'=2,'tp'=2] {'seq'}, dimensions={0}, use_global_device_ids=true | all-gather | bytes 737280 | tf_op jit(solution)/shard_map/all_gather | solution.py:30
  213.1 0.4 reshape.94
  213.5 0.9 copy.30
  214.4 16.1 %all_gather.19 = bf16[1024,288]{0,1:T(8,128)(2,1)S(1)} all-gather(bf16[256,288]{0,1:T(8,128)(2,1)S(1)} %get-tuple-element.100), channel_id=1, replica_groups=mesh['groups'=2,'seq'=4,'exp'=2,'tp'=2] {'seq'}, dimensions={0}, use_global_device_ids=true | all-gather | bytes 737280 | tf_op jit(solution)/shard_map/all_gather | solution.py:31
  230.5 0.4 reshape.96
  230.9 0.9 copy.31
  231.9 2.1 add_convert_fusion
  234.0 4.9 %all-to-all-start.1 = ((bf16[4,80,1152]{2,1,0:T(8,128)(2,1)}), bf16[4,80,1152]{2,1,0:T(8,128)(2,1)S(1)}, u32[]{:S(2)}, u32[]{:S(2)}) async-start(bf16[4,80,1152]{2,1,0:T(8,128)(2,1)} %bitcast.10), calls=%async_computation.2 | async-start | bytes 1474560 | tf_op jit(solution)/shard_map/all_to_all | solution.py:109
  238.8 6.9 %while.15 = (s32[]{:T(128)}, f32[4,256]{1,0:T(4,128)S(1)}, f32[4,256]{1,0:T(4,128)S(1)}, f32[4,256,72]{1,2,0:T(8,128)S(1)}, bf16[2,512,4,72]{1,3,2,0:T(8,128)(2,...) while((s32[]{:T(128)}, f32[4,256]{1,0:T(4,128)S(1)}, ...), condition=%wide.region_3.4_spmd.clone, body=%wide.region_0.3_spmd.clone.sunk | while | flops 155415552 | bytes 7685225 | solution.py:57
  238.8 1.5 bitcast_reduce_fusion.2
  240.4 0.4 fusion.49
  240.8 1.5 convolution_add_fusion.2
  242.3 1.5 bitcast_reduce_fusion.2
  243.8 0.4 fusion.49
  244.2 1.5 convolution_add_fusion.2
  246.0 0.7 divide_convert_fusion
  246.7 4.9 %all-to-all-done.1 = bf16[4,80,1152]{2,1,0:T(8,128)(2,1)S(1)} async-done(((bf16[4,80,1152]{2,1,0:T(8,128)(2,1)}), bf16[4,80,1152]{2,1,0:T(8,128)(2,1)S(1)}, u32[]{:S(2)}, u32[]{:S(2)}) %all-to-all-start.1) | async-done | bytes 737312 | tf_op jit(solution)/shard_map/all_to_all | solution.py:109
  251.6 1.3 gather_fusion
  252.8 0.6 reshape.103
  253.4 2.2 multiply_reduce_fusion
  (58 shorter events, 1.7 us)
Async XLA Ops:
  7.2 3.1 %copy-start = (bf16[128,1152]{1,0:T(8,128)(2,1)S(1)}, bf16[128,1152]{1,0:T(8,128)(2,1)}, u32[]{:S(2)}) copy-start(bf16[128,1152]{1,0:T(8,128)(2,1)} %param.21) | copy-start | bytes 884740
  7.2 37.7 %all-gather.6.cloned.1.call-start = ((), (), s32[]{:S(2)}) async-start(), calls=%async_computation.3 | async-start | bytes 2211840 | tf_op jit(solution)/shard_map/all_gather | solution.py:88
  36.0 1.5 copy-start.5
  36.0 80.9 %all-gather.8.cloned.1.call-start = ((), (), s32[]{:S(2)}) async-start(), calls=%async_computation.5 | async-start | bytes 7962624 | tf_op jit(solution)/shard_map/all_gather | solution.py:11
  36.7 151.0 %all-gather.10.cloned.1.call-start = ((), (), s32[]{:S(2)}) async-start(), calls=%async_computation.6 | async-start | bytes 7962624 | tf_op jit(solution)/shard_map/all_gather | solution.py:101
  37.5 194.4 %reduce-scatter.2.cloned.1.call-start = ((), (), s32[]{:S(2)}) async-start(), calls=%async_computation.4 | async-start | bytes 2211840 | tf_op jit(solution)/shard_map/reduce_scatter | solution.py:102
  126.5 69.9 %copy-start.8 = (s32[2]{0:T(128)S(1)}, s32[2]{0:T(128)}, u32[]{:S(2)}) copy-start(s32[2]{0:T(128)} %param.20) | copy-start | bytes 28
  126.5 70.0 %copy-start.1 = (bf16[256,288]{0,1:T(8,128)(2,1)S(1)}, bf16[256,288]{0,1:T(8,128)(2,1)}, u32[]{:S(2)}) copy-start(bf16[256,288]{0,1:T(8,128)(2,1)} %param.17) | copy-start | bytes 442372
  126.5 70.0 %copy-start.2 = (bf16[256,288]{0,1:T(8,128)(2,1)S(1)}, bf16[256,288]{0,1:T(8,128)(2,1)}, u32[]{:S(2)}) copy-start(bf16[256,288]{0,1:T(8,128)(2,1)} %param.19) | copy-start | bytes 442372
  126.5 70.0 %copy-start.3 = (bf16[256,288]{0,1:T(8,128)(2,1)S(1)}, bf16[256,288]{0,1:T(8,128)(2,1)}, u32[]{:S(2)}) copy-start(bf16[256,288]{0,1:T(8,128)(2,1)} %param.16) | copy-start | bytes 442372
  126.5 70.0 %copy-start.4 = (bf16[256,288]{0,1:T(8,128)(2,1)S(1)}, bf16[256,288]{0,1:T(8,128)(2,1)}, u32[]{:S(2)}) copy-start(bf16[256,288]{0,1:T(8,128)(2,1)} %param.18) | copy-start | bytes 442372
  213.1 18.7 %copy-start.6 = (f32[1,1152]{1,0:T(1,128)S(1)}, f32[1,1152]{1,0:T(1,128)}, u32[]{:S(2)}) copy-start(f32[1,1152]{1,0:T(1,128)} %param.27) | copy-start | bytes 13828
  234.0 17.6 %all-to-all-start.1 = ((bf16[4,80,1152]{2,1,0:T(8,128)(2,1)}), bf16[4,80,1152]{2,1,0:T(8,128)(2,1)S(1)}, u32[]{:S(2)}, u32[]{:S(2)}) async-start(bf16[4,80,1152]{2,1,0:T(8,128)(2,1)} %bitcast.10), calls=%async_computation.2 | async-start | bytes 1474560 | tf_op jit(solution)/shard_map/all_to_all | solution.py:109
  238.8 7.0 %copy-start.7 = (f32[128,2]{0,1:T(2,128)S(1)}, f32[128,2]{0,1:T(2,128)}, u32[]{:S(2)}) copy-start(f32[128,2]{0,1:T(2,128)} %param.23) | copy-start | bytes 3076
Sparse Core Ops, SparseCore 0:
  36.1 8.7 all-gather.5
  46.4 70.4 all-gather.7
  118.5 69.2 all-gather.9
  196.5 8.9 reduce-scatter.1
where the time goes:
time: 263 us; the launch traced here: 262 us
  waiting for transfers between devices  143 us (54%)
  blocking collectives  62.3 us (24%)
  matrix products  24.4 us (9%)
  between operations  14 us (5%)
  other arithmetic  7.3 us (3%)
  local copies, waits for them, and re-layouts  6.41 us (2%)
  starting transfers between devices  5.02 us (2%)
    all_gather x1, waiting for transfers between devices, over_all_2(): everything = lax.all_gather(share, axis, axis=dim, tiled=True)  72 us
    all_gather x1, waiting for transfers between devices, expert_part(): down_whole = lax.all_gather(down_weight[0], 'exp', axis=0, tiled=True)  61.3 us
    all_to_all x1, blocking collectives, expert_part(): lax.all_to_all(buffer, 'seq', split_axis=0, concat_axis=0, tiled=True)  25.3 us
    all_gather x1, blocking collectives, attention_part(): lax.all_gather(keys, 'seq', axis=0, tiled=True)  16.5 us
    all_gather x1, blocking collectives, attention_part(): lax.all_gather(values, 'seq', axis=0, tiled=True)  16.1 us
    dot_general x1, matrix products, project(): jnp.dot(chip_rows, piece[0], preferred_element_type=jnp.float32) + piece[1]  9.57 us
    dot_general x1, matrix products, expert_part(): jnp.dot(hidden, down_whole, preferred_element_type=jnp.float32)  8.54 us
  transfers between devices with their start and end apart: 5, of which 4 were waited for; matrix products, arithmetic and copies ran while one was open for 8% of the time, Pallas kernels for 0%

commit v1 on v0

--- a/solution.py
+++ b/solution.py
@@ -5,6 +5,27 @@
 from jax.sharding import PartitionSpec as P
 
 HD = 72
+
+
+def joined_along(blocks, dim):
+    blocks = jnp.moveaxis(blocks, 0, dim)
+    dims = blocks.shape
+    return blocks.reshape(*dims[:dim], dims[dim] * dims[dim + 1], *dims[dim + 2 :])
+
+
+def grow_blocks(array, axis):
+    length, index = (lax.axis_size(axis), lax.axis_index(axis))
+    blocks, stride = (array[None], 1)
+    while stride < length:
+        theirs = lax.ppermute(blocks, axis, [(i, i ^ stride) for i in range(length)])
+        low = index & stride == 0
+        blocks = jnp.concatenate([jnp.where(low, blocks, theirs), jnp.where(low, theirs, blocks)])
+        stride *= 2
+    return blocks
+
+
+def gather_by_bits(x, axis, dim):
+    return joined_along(grow_blocks(x, axis), dim)
 
 
 def over_all_2(share, axis, dim, apply):
@@ -26,10 +47,7 @@
         jnp.zeros((heads_here, length, HD), jnp.float32),
     )
     carry = initial
-    piece = (
-        lax.all_gather(keys, "seq", axis=0, tiled=True),
-        lax.all_gather(values, "seq", axis=0, tiled=True),
-    )
+    piece = (lax.all_gather(keys, "seq", axis=0, tiled=True), gather_by_bits(values, "seq", 0))
     count = piece[0].shape[0]
     width = math.gcd(count, 512)
     key_blocks = piece[0].reshape(count // width, width, heads_here, HD)

time: 263 us -> 266 us (1.011)
  waiting for transfers between devices: 143 us -> 159 us
  blocking collectives: 62.3 us -> 47 us
    all_gather x1 -> x0, blocking collectives: 16.1 us -> none  [attention_part(): lax.all_gather(values, 'seq', axis=0, tiled=True)]
    ppermute x0 -> x2, waiting for transfers between devices: none -> 11.3 us  [grow_blocks(): lax.ppermute(blocks, axis, [(i, i ^ stride) for i in range(length)])]
    all_to_all x1, waiting for transfers between devices: 4.88 us -> 10.3 us  [expert_part(): lax.all_to_all(result, 'seq', split_axis=0, concat_axis=0, tiled=True)]
  transfers between devices with their start and end apart: 5 -> 7, of which waited for: 4 -> 5; matrix products, arithmetic and copies ran while one was open for 8% -> 8% of each run, Pallas kernels for 0% -> 0%
where the time goes in v1:
time: 266 us; the launch traced here: 265 us
  waiting for transfers between devices  159 us (60%)
  blocking collectives  47 us (18%)
  matrix products  24.4 us (9%)
  between operations  14 us (5%)
  other arithmetic  7.48 us (3%)
  local copies, waits for them, and re-layouts  6.81 us (3%)
  starting transfers between devices  6.2 us (2%)
    all_gather x1, waiting for transfers between devices, over_all_2(): everything = lax.all_gather(share, axis, axis=dim, tiled=True)  72 us
    all_gather x1, waiting for transfers between devices, expert_part(): down_whole = lax.all_gather(down_weight[0], 'exp', axis=0, tiled=True)  61.2 us
    all_to_all x1, blocking collectives, expert_part(): lax.all_to_all(buffer, 'seq', split_axis=0, concat_axis=0, tiled=True)  25.3 us
    all_gather x1, blocking collectives, attention_part(): lax.all_gather(keys, 'seq', axis=0, tiled=True)  17.3 us
    ppermute x2, waiting for transfers between devices, grow_blocks(): lax.ppermute(blocks, axis, [(i, i ^ stride) for i in range(length)])  11.3 us
    all_to_all x1, waiting for transfers between devices, expert_part(): lax.all_to_all(result, 'seq', split_axis=0, concat_axis=0, tiled=True)  10.3 us
    dot_general x1, matrix products, project(): jnp.dot(chip_rows, piece[0], preferred_element_type=jnp.float32) + piece[1]  9.58 us
    dot_general x1, matrix products, expert_part(): jnp.dot(hidden, down_whole, preferred_element_type=jnp.float32)  8.54 us
  transfers between devices with their start and end apart: 7, of which 5 were waited for; matrix products, arithmetic and copies ran while one was open for 8% of the time, Pallas kernels for 0%

profile of v1, /device:TPU:0, one launch (start us, length us, event | category | flops | bytes accessed | tf_op | source)
XLA Modules:
  0.0 265.3 jit_solution(3433209990215338623)
XLA Ops:
  7.2 0.8 copy.34
  8.3 1.2 reduce-window.6
  10.6 25.3 %all_to_all.10 = bf16[4,80,1152]{2,1,0:T(8,128)(2,1)} all-to-all(bf16[4,80,1152]{2,1,0:T(8,128)(2,1)S(1)} %bitcast.84), channel_id=1, replica_groups=mesh['groups'=2,'seq'=4,'exp'=2,'tp'=2] {'seq'}, dimensions={0} | all-to-all | bytes 1474560 | tf_op jit(solution)/shard_map/all_to_all | solution.py:102
  36.0 0.7 all-gather.8.cloned.1.call-update
  36.8 0.7 all-gather.10.cloned.1.call-update
  37.5 4.4 %all_gather.18 = bf16[1,2304]{1,0:T(2,128)(2,1)S(1)} all-gather(bf16[1,1152]{1,0:T(2,128)(2,1)S(1)} %convert_element_type.61), channel_id=1, replica_groups=mesh['groups'=2,'seq'=4,'exp'=2,'tp'=2] {'exp'}, dimensions={1}, use_global_device_ids=true | all-gather | bytes 6912 | tf_op jit(solution)/shard_map/all_gather | solution.py:32
  41.9 3.0 %all-gather.6.cloned.1.call-done = bf16[640,1152]{1,0:T(8,128)(2,1)} async-done(((bf16[320,1152]{1,0:T(8,128)(2,1)}), bf16[640,1152]{1,0:T(8,128)(2,1)}) %all-gather.6.cloned.1.call-update) | async-done | bytes 1474576 | tf_op jit(solution)/shard_map/all_gather | solution.py:106
  44.9 72.0 %all-gather.8.cloned.1.call-done = bf16[1,1152,2304]{2,1,0:T(8,128)(2,1)} async-done(((bf16[1,1152,1152]{2,1,0:T(8,128)(2,1)}), bf16[1,1152,2304]{2,1,0:T(8,128)(2,1)}) %all-gather.8.cloned.1.call-update) | async-done | bytes 5308432 | tf_op jit(solution)/shard_map/all_gather | solution.py:32
  116.9 9.6 %fusion.22 = bf16[640,2304]{1,0:T(8,128)(2,1)} fusion(bf16[640,1152]{1,0:T(8,128)(2,1)} %all-gather.6.cloned.1.call-done, bf16[1,1152,2304]{2,1,0:T(8,128)(2,1)} %all-gather.8.cloned.1.call-done, f32[2304]{0:T(1024)S(1)} %convert_reduce_fusion.1), kind=kOutput, calls=%fused_computation.30 | convolution fusion | flops 3412131840 | bytes 9741312 | tf_op jit(solution)/shard_map/dot_general | solution.py:110
  126.5 61.2 %all-gather.10.cloned.1.call-done = bf16[1,2304,1152]{2,1,0:T(8,128)(2,1)} async-done(((bf16[1,1152,1152]{2,1,0:T(8,128)(2,1)}), bf16[1,2304,1152]{2,1,0:T(8,128)(2,1)}) %all-gather.10.cloned.1.call-update) | async-done | bytes 5308432 | tf_op jit(solution)/shard_map/all_gather | solution.py:119
  187.8 8.5 %fusion.29 = bf16[640,1152]{1,0:T(8,128)(2,1)} fusion(bf16[640,2304]{1,0:T(8,128)(2,1)} %fusion.22, bf16[1,2304,1152]{2,1,0:T(8,128)(2,1)} %all-gather.10.cloned.1.call-done), kind=kOutput, calls=%fused_computation.35 | convolution fusion | flops 3398123520 | bytes 9732096 | tf_op jit(solution)/shard_map/dot_general | solution.py:121
  196.5 1.6 collective-permute-start
  198.1 17.3 %all_gather.15 = bf16[1024,288]{0,1:T(8,128)(2,1)S(1)} all-gather(bf16[256,288]{0,1:T(8,128)(2,1)S(1)} %get-tuple-element.105), channel_id=1, replica_groups=mesh['groups'=2,'seq'=4,'exp'=2,'tp'=2] {'seq'}, dimensions={0}, use_global_device_ids=true | all-gather | bytes 737280 | tf_op jit(solution)/shard_map/all_gather | solution.py:50
  215.4 0.4 reshape.91
  215.8 0.9 copy.32
  217.1 0.8 collective-permute-start.1
  217.9 11.3 %collective-permute-done.1 = bf16[2,256,288]{1,2,0:T(8,128)(2,1)S(1)} collective-permute-done((bf16[2,256,288]{1,2,0:T(8,128)(2,1)S(1)}, bf16[2,256,288]{1,2,0:T(8,128)(2,1)S(1)}, u32[]{:S(2)}, u32[]{:S(2)}) %collective-permute-start.1) | collective-permute-done | bytes 294944 | tf_op jit(solution)/shard_map/ppermute | solution.py:20
  229.3 0.5 copy.31
  229.8 0.4 reshape_reshape.3
  230.2 0.9 copy.33
  231.0 2.1 add_convert_fusion
  233.2 3.7 %all-to-all-start.1 = ((bf16[4,80,1152]{2,1,0:T(8,128)(2,1)}), bf16[4,80,1152]{2,1,0:T(8,128)(2,1)S(1)}, u32[]{:S(2)}, u32[]{:S(2)}) async-start(bf16[4,80,1152]{2,1,0:T(8,128)(2,1)} %bitcast.11), calls=%async_computation.2 | async-start | bytes 1474560 | tf_op jit(solution)/shard_map/all_to_all | solution.py:127
  236.8 6.9 %while.15 = (s32[]{:T(128)}, f32[4,256]{1,0:T(4,128)S(1)}, f32[4,256]{1,0:T(4,128)S(1)}, f32[4,256,72]{1,2,0:T(8,128)S(1)}, bf16[2,512,4,72]{1,3,2,0:T(8,128)(2,...) while((s32[]{:T(128)}, f32[4,256]{1,0:T(4,128)S(1)}, ...), condition=%wide.region_3.4_spmd.clone, body=%wide.region_0.3_spmd.clone.sunk | while | flops 155415552 | bytes 7685225 | solution.py:75
  236.8 1.5 bitcast_reduce_fusion.2
  238.8 1.5 convolution_add_fusion.2
  240.3 1.5 bitcast_reduce_fusion.2
  242.2 1.5 convolution_add_fusion.2
  243.7 0.7 divide_convert_fusion
  244.4 10.3 %all-to-all-done.1 = bf16[4,80,1152]{2,1,0:T(8,128)(2,1)S(1)} async-done(((bf16[4,80,1152]{2,1,0:T(8,128)(2,1)}), bf16[4,80,1152]{2,1,0:T(8,128)(2,1)S(1)}, u32[]{:S(2)}, u32[]{:S(2)}) %all-to-all-start.1) | async-done | bytes 737312 | tf_op jit(solution)/shard_map/all_to_all | solution.py:127
  254.7 1.3 gather_fusion
  256.0 0.6 reshape.99
  256.6 2.2 multiply_reduce_fusion
  (66 shorter events, 2.9 us)
Async XLA Ops:
  7.2 3.1 %copy-start = (bf16[128,1152]{1,0:T(8,128)(2,1)S(1)}, bf16[128,1152]{1,0:T(8,128)(2,1)}, u32[]{:S(2)}) copy-start(bf16[128,1152]{1,0:T(8,128)(2,1)} %param.21) | copy-start | bytes 884740
  7.2 37.7 %all-gather.6.cloned.1.call-start = ((), (), s32[]{:S(2)}) async-start(), calls=%async_computation.3 | async-start | bytes 2211840 | tf_op jit(solution)/shard_map/all_gather | solution.py:106
  36.0 1.5 copy-start.5
  36.0 80.9 %all-gather.8.cloned.1.call-start = ((), (), s32[]{:S(2)}) async-start(), calls=%async_computation.5 | async-start | bytes 7962624 | tf_op jit(solution)/shard_map/all_gather | solution.py:32
  36.7 151.0 %all-gather.10.cloned.1.call-start = ((), (), s32[]{:S(2)}) async-start(), calls=%async_computation.6 | async-start | bytes 7962624 | tf_op jit(solution)/shard_map/all_gather | solution.py:119
  37.5 193.6 %reduce-scatter.2.cloned.1.call-start = ((), (), s32[]{:S(2)}) async-start(), calls=%async_computation.4 | async-start | bytes 2211840 | tf_op jit(solution)/shard_map/reduce_scatter | solution.py:120
  126.5 69.8 %copy-start.8 = (s32[2]{0:T(128)S(1)}, s32[2]{0:T(128)}, u32[]{:S(2)}) copy-start(s32[2]{0:T(128)} %param.20) | copy-start | bytes 28
  126.5 69.9 %copy-start.1 = (bf16[256,288]{0,1:T(8,128)(2,1)S(1)}, bf16[256,288]{0,1:T(8,128)(2,1)}, u32[]{:S(2)}) copy-start(bf16[256,288]{0,1:T(8,128)(2,1)} %param.17) | copy-start | bytes 442372
  126.5 69.9 %copy-start.2 = (bf16[256,288]{0,1:T(8,128)(2,1)S(1)}, bf16[256,288]{0,1:T(8,128)(2,1)}, u32[]{:S(2)}) copy-start(bf16[256,288]{0,1:T(8,128)(2,1)} %param.19) | copy-start | bytes 442372
  126.5 69.9 %copy-start.3 = (bf16[256,288]{0,1:T(8,128)(2,1)S(1)}, bf16[256,288]{0,1:T(8,128)(2,1)}, u32[]{:S(2)}) copy-start(bf16[256,288]{0,1:T(8,128)(2,1)} %param.16) | copy-start | bytes 442372
  126.5 69.9 %copy-start.4 = (bf16[256,288]{0,1:T(8,128)(2,1)S(1)}, bf16[256,288]{0,1:T(8,128)(2,1)}, u32[]{:S(2)}) copy-start(bf16[256,288]{0,1:T(8,128)(2,1)} %param.18) | copy-start | bytes 442372
  196.3 20.5 %copy-start.7 = (f32[128,2]{0,1:T(2,128)S(1)}, f32[128,2]{0,1:T(2,128)}, u32[]{:S(2)}) copy-start(f32[128,2]{0,1:T(2,128)} %param.23) | copy-start | bytes 3076
  196.3 20.7 %copy-start.6 = (f32[1,1152]{1,0:T(1,128)S(1)}, f32[1,1152]{1,0:T(1,128)}, u32[]{:S(2)}) copy-start(f32[1,1152]{1,0:T(1,128)} %param.27) | copy-start | bytes 13828
  196.5 20.5 %collective-permute-start = (bf16[1,256,288]{1,2,0:T(8,128)(2,1)S(1)}, bf16[1,256,288]{1,2,0:T(8,128)(2,1)S(1)}, u32[]{:S(2)}, u32[]{:S(2)}) collective-permute-start(bf16[1,256,288]{1,2,0:T(8,128)(2,1)S(1)} %get-tuple-element.104), channel_id=1, source_target_pairs={{0,4},{4,0},{8,12},{12,8},{1,5},{5,1},{9,13},{13,9},{2,6},{6,2},{1... | collective-permute-start | bytes 442376 | tf_op jit(solution)/shard_map/ppermute | solution.py:20
  217.1 12.1 %collective-permute-start.1 = (bf16[2,256,288]{1,2,0:T(8,128)(2,1)S(1)}, bf16[2,256,288]{1,2,0:T(8,128)(2,1)S(1)}, u32[]{:S(2)}, u32[]{:S(2)}) collective-permute-start(bf16[2,256,288]{1,2,0:T(8,128)(2,1)S(1)} %pad_maximum_fusion.1), channel_id=1, source_target_pairs={{0,8},{4,12},{8,0},{12,4},{1,9},{5,13},{9,1},{13,5},{2,10},{6,14},... | collective-permute-start | bytes 884744 | tf_op jit(solution)/shard_map/ppermute | solution.py:20
  233.2 21.6 %all-to-all-start.1 = ((bf16[4,80,1152]{2,1,0:T(8,128)(2,1)}), bf16[4,80,1152]{2,1,0:T(8,128)(2,1)S(1)}, u32[]{:S(2)}, u32[]{:S(2)}) async-start(bf16[4,80,1152]{2,1,0:T(8,128)(2,1)} %bitcast.11), calls=%async_computation.2 | async-start | bytes 1474560 | tf_op jit(solution)/shard_map/all_to_all | solution.py:127
Sparse Core Ops, SparseCore 0:
  36.1 8.7 all-gather.5
  46.4 70.4 all-gather.7
  118.5 69.2 all-gather.9
  196.5 8.8 reduce-scatter.1
